TPU v7x, 32 devices: a whole 2x2x4 slice. The times are simulated.
32 devices in a mesh: outer: 8 (over z, x), inner: 4 (over y, core).
Axes of the slice: x: 2, y: 2, z: 4, core: 2. Of those that a mesh axis runs over, the one named last changes fastest.
Arguments:
- queries: bfloat16 [1024, 2, 4096], P('outer', None, 'inner'), may hold values from -52 to 52
- keys: bfloat16 [1024, 2, 4096], P('outer', None, 'inner'), may hold values from -6 to 6
- values: bfloat16 [1024, 2, 4096], P('outer', None, 'inner'), may hold values from -6 to 6
Outputs:
- attended: bfloat16 [1024, 2, 4096], P(('outer', 'inner'))
All inputs are finite; a program needn't handle non-finite values.
Results may differ from a plain program's by a relative error of at most 0.004.
Values may be sent and summed in bfloat16 or wider, within the bound.
A program may use at most 128 MiB of HBM per device.

v0:
```python
from functools import partial
import math
import jax
import jax.numpy as jnp
from jax import lax
from jax.sharding import PartitionSpec as P

HEAD_DIM = 128


def attend_keys(running, key_block, value_block, query_heads, head_count):
    peak_rows, totals, numerator = running
    key_count = key_block.shape[0]
    key_heads = key_block.reshape(key_count, head_count, HEAD_DIM)
    value_heads = value_block.reshape(key_count, head_count, HEAD_DIM)
    scores = jnp.einsum(
        "qhd,khd->qhk", query_heads, key_heads, preferred_element_type=jnp.float32
    ) * (1.0 / math.sqrt(HEAD_DIM))
    new_peaks = jnp.maximum(peak_rows, jnp.max(scores, axis=2))
    shrink = jnp.exp(peak_rows - new_peaks)
    weights = jnp.exp(scores - new_peaks[..., None])
    totals = totals * shrink + jnp.sum(weights, axis=2)
    numerator = numerator * shrink[..., None] + jnp.einsum(
        "qhk,khd->qhd",
        weights.astype(jnp.bfloat16),
        value_heads,
        preferred_element_type=jnp.float32,
    )
    return (new_peaks, totals, numerator)


def attend_piece(running, pieces, start_row, query_part, head_count):
    key_rows, value_rows = pieces
    row_count = query_part.shape[0]
    query_heads = query_part.reshape(row_count, head_count, HEAD_DIM)
    block_count = key_rows.shape[0] // row_count
    key_blocks = key_rows.reshape(block_count, row_count, key_rows.shape[1])
    value_blocks = value_rows.reshape(block_count, row_count, value_rows.shape[1])

    def one_block(state, blocks):
        return (attend_keys(state, blocks[0], blocks[1], query_heads, head_count), None)

    running, unused = lax.scan(one_block, running, (key_blocks, value_blocks))
    return running


def start_state(row_count, head_count):
    peak_rows = jnp.full((row_count, head_count), -1e30, jnp.float32)
    totals = jnp.zeros((row_count, head_count), jnp.float32)
    numerator = jnp.zeros((row_count, head_count, HEAD_DIM), jnp.float32)
    return (peak_rows, totals, numerator)


def finish_state(running):
    peak_rows, totals, numerator = running
    averaged = numerator / totals[..., None]
    return averaged.reshape(numerator.shape[0], -1).astype(jnp.bfloat16)


def flatten(array):
    return array.reshape(array.shape[0], array.shape[1] * array.shape[2])


def per_device(queries, keys, values):
    tok_rows, networks, local_cols = queries.shape
    full_q, full_k, full_v = (
        lax.all_to_all(queries, "inner", split_axis=0, concat_axis=2, tiled=True),
        lax.all_to_all(keys, "inner", split_axis=0, concat_axis=2, tiled=True),
        lax.all_to_all(values, "inner", split_axis=0, concat_axis=2, tiled=True),
    )
    unit_rows = full_q.shape[0]
    full_cols = full_q.shape[2]
    query_part, key_part, value_part = (
        lax.all_to_all(flatten(full_q), "outer", split_axis=1, concat_axis=0, tiled=True),
        lax.all_to_all(flatten(full_k), "outer", split_axis=1, concat_axis=0, tiled=True),
        lax.all_to_all(flatten(full_v), "outer", split_axis=1, concat_axis=0, tiled=True),
    )
    head_count = query_part.shape[1] // HEAD_DIM
    folder = partial(attend_piece, query_part=query_part, head_count=head_count)
    running = folder(
        start_state(query_part.shape[0], head_count),
        (
            lax.all_gather(key_part, "inner", axis=0, tiled=True),
            lax.all_gather(value_part, "inner", axis=0, tiled=True),
        ),
        jnp.int32(0),
    )
    gathered = lax.all_to_all(
        finish_state(running), "outer", split_axis=0, concat_axis=1, tiled=True
    )
    attended = gathered.reshape(unit_rows, networks, full_cols)
    return attended


def solution(mesh):
    return jax.shard_map(
        per_device,
        mesh=mesh,
        in_specs=(P("outer", None, "inner"), P("outer", None, "inner"), P("outer", None, "inner")),
        out_specs=P(("outer", "inner"), None, None),
        check_vma=False,
    )
```

profile of v0, /device:TPU:0, one launch (start us, length us, event | category | flops | bytes accessed | tf_op | source)
XLA Modules:
  0.0 146.4 jit_solution(7811544565537679665)
XLA Ops:
  6.5 13.2 %all_to_all.112 = bf16[128,2,1024]{2,1,0:T(2,128)(2,1)S(1)} all-to-all(bf16[128,2,1024]{2,1,0:T(2,128)(2,1)} %param.6), channel_id=1, replica_groups=mesh['outer'=8,'inner'=4] {'inner'}, dimensions={0} | all-to-all | bytes 1048576 | tf_op jit(solution)/shard_map/all_to_all | solution.py:68
  19.9 20.5 %all_to_all.113 = bf16[32,8,1024]{2,0,1:T(8,128)(2,1)} all-to-all(bf16[32,8,1024]{2,0,1:T(8,128)(2,1)S(1)} %bitcast.72), channel_id=1, replica_groups=mesh['outer'=8,'inner'=4] {'outer'}, dimensions={1} | all-to-all | bytes 1048576 | tf_op jit(solution)/shard_map/all_to_all | solution.py:75
  40.4 14.9 %all_to_all.114 = bf16[128,2,1024]{2,1,0:T(2,128)(2,1)S(1)} all-to-all(bf16[128,2,1024]{2,1,0:T(2,128)(2,1)S(1)} %copy-done), channel_id=1, replica_groups=mesh['outer'=8,'inner'=4] {'inner'}, dimensions={0} | all-to-all | bytes 1048576 | tf_op jit(solution)/shard_map/all_to_all | solution.py:69
  55.5 17.2 %all_to_all.115 = bf16[32,8,1024]{2,0,1:T(8,128)(2,1)} all-to-all(bf16[32,8,1024]{2,0,1:T(8,128)(2,1)S(1)} %bitcast.73), channel_id=1, replica_groups=mesh['outer'=8,'inner'=4] {'outer'}, dimensions={1} | all-to-all | bytes 1048576 | tf_op jit(solution)/shard_map/all_to_all | solution.py:76
  72.7 14.9 %all_to_all.116 = bf16[128,2,1024]{2,1,0:T(2,128)(2,1)S(1)} all-to-all(bf16[128,2,1024]{2,1,0:T(2,128)(2,1)S(1)} %copy-done.1), channel_id=1, replica_groups=mesh['outer'=8,'inner'=4] {'inner'}, dimensions={0} | all-to-all | bytes 1048576 | tf_op jit(solution)/shard_map/all_to_all | solution.py:67
  87.5 0.9 copy.17
  88.5 3.5 %all-to-all-start.3 = ((bf16[32,8,1024]{2,0,1:T(8,128)(2,1)}), bf16[32,8,1024]{2,0,1:T(8,128)(2,1)S(1)}, u32[]{:S(2)}, u32[]{:S(2)}) async-start(bf16[32,8,1024]{2,0,1:T(8,128)(2,1)} %bitcast.8), calls=%async_computation.3 | async-start | bytes 1048576 | tf_op jit(solution)/shard_map/all_to_all | solution.py:74
  92.0 14.0 %all-to-all-done.3 = bf16[32,8,1024]{2,0,1:T(8,128)(2,1)S(1)} async-done(((bf16[32,8,1024]{2,0,1:T(8,128)(2,1)}), bf16[32,8,1024]{2,0,1:T(8,128)(2,1)S(1)}, u32[]{:S(2)}, u32[]{:S(2)}) %all-to-all-start.3) | async-done | bytes 524320 | tf_op jit(solution)/shard_map/all_to_all | solution.py:74
  106.3 13.4 %while.15 = (s32[]{:T(128)}, f32[256,8]{0,1:T(8,128)S(1)}, f32[256,8]{0,1:T(8,128)S(1)}, f32[256,8,128]{0,2,1:T(8,128)S(1)}, bf16[4,256,1024]{2,1,0:T(8,128)(2,1...) while((s32[]{:T(128)}, f32[256,8]{0,1:T(8,128)S(1)}, ...), condition=%wide.region_3.4_spmd.clone, body=%wide.region_0.3_spmd.clone.sunk | while | flops 273426432 | bytes 14286965 | solution.py:43
  106.3 1.3 constant_dynamic-slice_fusion.3
  108.0 0.5 bitcast_reduce_fusion.2
  108.5 0.4 fusion.23
  108.9 0.7 fusion.25
  109.6 1.3 constant_dynamic-slice_fusion.3
  111.3 0.5 bitcast_reduce_fusion.2
  112.2 0.7 fusion.25
  113.0 1.3 constant_dynamic-slice_fusion.3
  114.7 0.5 bitcast_reduce_fusion.2
  115.6 0.7 fusion.25
  116.3 1.3 constant_dynamic-slice_fusion.3
  118.0 0.5 bitcast_reduce_fusion.2
  118.9 0.7 fusion.25
  120.3 17.9 %all_to_all.117 = bf16[8,32,1024]{2,1,0:T(8,128)(2,1)S(1)} all-to-all(bf16[8,32,1024]{2,1,0:T(8,128)(2,1)S(1)} %convert_element_type.11), channel_id=1, replica_groups=mesh['outer'=8,'inner'=4] {'outer'}, dimensions={0} | all-to-all | bytes 1048576 | tf_op jit(solution)/shard_map/all_to_all | solution.py:88
  138.5 1.1 reshape.52
  (44 shorter events, 4.2 us)
Async XLA Ops:
  6.5 33.9 %copy-start = (bf16[128,2,1024]{2,1,0:T(2,128)(2,1)S(1)}, bf16[128,2,1024]{2,1,0:T(2,128)(2,1)}, u32[]{:S(2)}) copy-start(bf16[128,2,1024]{2,1,0:T(2,128)(2,1)} %param.7) | copy-start | bytes 1572868
  6.5 99.7 %all-gather.3.cloned.1.call-start = ((), (), s32[]{:S(2)}) async-start(), calls=%async_computation.7 | async-start | bytes 2621440 | tf_op jit(solution)/shard_map/all_gather | solution.py:83
  40.3 32.3 %copy-start.1 = (bf16[128,2,1024]{2,1,0:T(2,128)(2,1)S(1)}, bf16[128,2,1024]{2,1,0:T(2,128)(2,1)}, u32[]{:S(2)}) copy-start(bf16[128,2,1024]{2,1,0:T(2,128)(2,1)} %param.5) | copy-start | bytes 1572868
  40.4 65.9 %all-gather.5.cloned.1.call-start = ((), (), s32[]{:S(2)}) async-start(), calls=%async_computation.8 | async-start | bytes 2621440 | tf_op jit(solution)/shard_map/all_gather | solution.py:84
  88.5 17.6 %all-to-all-start.3 = ((bf16[32,8,1024]{2,0,1:T(8,128)(2,1)}), bf16[32,8,1024]{2,0,1:T(8,128)(2,1)S(1)}, u32[]{:S(2)}, u32[]{:S(2)}) async-start(bf16[32,8,1024]{2,0,1:T(8,128)(2,1)} %bitcast.8), calls=%async_computation.3 | async-start | bytes 1048576 | tf_op jit(solution)/shard_map/all_to_all | solution.py:74
Sparse Core Ops, SparseCore 0:
  40.5 24.0 all-gather.2
  72.8 23.8 all-gather.4
where the time goes:
time: 147 us; the launch traced here: 146 us
  blocking collectives  98.5 us (67%)
  waiting for transfers between devices  14.1 us (10%)
  between operations  13.5 us (9%)
  local copies, waits for them, and re-layouts  10 us (7%)
  matrix products  4.86 us (3%)
  starting transfers between devices  3.54 us (2%)
  other arithmetic  1.62 us (1%)
    all_to_all x1, blocking collectives, per_device(): lax.all_to_all(flatten(full_k), 'outer', split_axis=1, concat_axis=0, til...  20.5 us
    all_to_all x1, blocking collectives, per_device(): lax.all_to_all(finish_state(running), 'outer', split_axis=0, concat_axis=...  17.9 us
    all_to_all x1, blocking collectives, per_device(): lax.all_to_all(flatten(full_v), 'outer', split_axis=1, concat_axis=0, til...  17.2 us
    all_to_all x1, blocking collectives, per_device(): lax.all_to_all(values, 'inner', split_axis=0, concat_axis=2, tiled=True)  14.9 us
    all_to_all x1, blocking collectives, per_device(): lax.all_to_all(queries, 'inner', split_axis=0, concat_axis=2, tiled=True)  14.9 us
    all_to_all x1, waiting for transfers between devices, per_device(): lax.all_to_all(flatten(full_q), 'outer', split_axis=1, concat_axis=0, til...  14 us
    all_to_all x1, blocking collectives, per_device(): lax.all_to_all(keys, 'inner', split_axis=0, concat_axis=2, tiled=True)  13.2 us
    dynamic_slice x12, local copies, waits for them, and re-layouts, attend_piece(): running, unused = lax.scan(one_block, running, (key_blocks, value_blocks))  6.72 us
  transfers between devices with their start and end apart: 3, of which 1 were waited for; matrix products, arithmetic and copies ran while one was open for 1% of the time, Pallas kernels for 0%

commit v1 on v0

--- a/solution.py
+++ b/solution.py
@@ -4,8 +4,22 @@
 import jax.numpy as jnp
 from jax import lax
 from jax.sharding import PartitionSpec as P
+from jax.lax import axis_index, axis_size, ppermute
 
 HEAD_DIM = 128
+
+
+def start_the_set(load, join_dim, incoming_x):
+    u1, res = (load.shape[:join_dim], load.shape[join_dim + 1 :])
+    outer = jnp.moveaxis(load.reshape(*u1, incoming_x, -1, *res), join_dim, 0)
+    return outer
+
+
+def point_grid(unit, dim_k):
+    before = list(unit.shape[1:])
+    before[dim_k] *= unit.shape[0]
+    near = jnp.moveaxis(unit, 0, dim_k).reshape(before)
+    return near
 
 
 def attend_keys(running, key_block, value_block, query_heads, head_count):
@@ -70,9 +84,21 @@
     )
     unit_rows = full_q.shape[0]
     full_cols = full_q.shape[2]
+
+    def proceed_inputs(inputs, comm_axis, obj, x_part):
+        t1, z2 = (axis_size(comm_axis), axis_index(comm_axis))
+        part_now = start_the_set(inputs, obj, t1)
+        ledger = [part_now[z2]]
+        for d in range(1, t1):
+            passed = part_now[(z2 + d) % t1]
+            ledger.append(ppermute(passed, comm_axis, [(p, (p + d) % t1) for p in range(t1)]))
+        part_now = jnp.stack(ledger)[(z2 - jnp.arange(t1)) % t1]
+        w2 = point_grid(part_now, x_part)
+        return w2
+
     query_part, key_part, value_part = (
         lax.all_to_all(flatten(full_q), "outer", split_axis=1, concat_axis=0, tiled=True),
-        lax.all_to_all(flatten(full_k), "outer", split_axis=1, concat_axis=0, tiled=True),
+        proceed_inputs(flatten(full_k), "outer", 1, 0),
         lax.all_to_all(flatten(full_v), "outer", split_axis=1, concat_axis=0, tiled=True),
     )
     head_count = query_part.shape[1] // HEAD_DIM

time: 147 us -> 158 us (1.075)
  blocking collectives: 98.5 us -> 66.8 us
  waiting for transfers between devices: 14.1 us -> 40.7 us
  starting transfers between devices: 3.54 us -> 18 us
    all_to_all x2 -> x0, blocking collectives: 33.7 us -> none  [the longest x1 20.5 us: per_device(): lax.all_to_all(flatten(full_k), 'outer', split_axis=1, concat_axis=0, til...]
    ppermute x0 -> x7, waiting for transfers between devices: none -> 17.8 us  [proceed_inputs(): ppermute(passed, comm_axis, [(p, (p + d) % t1) for p in range(t1)])]
    ppermute x0 -> x7, starting transfers between devices: none -> 10.2 us  [proceed_inputs(): ppermute(passed, comm_axis, [(p, (p + d) % t1) for p in range(t1)])]
    all_to_all x0 -> x1, waiting for transfers between devices: none -> 8.77 us  [per_device(): lax.all_to_all(keys, 'inner', split_axis=0, concat_axis=2, tiled=True)]
    all_to_all x0 -> x1, starting transfers between devices: none -> 4.26 us  [per_device(): lax.all_to_all(keys, 'inner', split_axis=0, concat_axis=2, tiled=True)]
    all_to_all x1, blocking collectives: 14.9 us -> 16.9 us  [per_device(): lax.all_to_all(values, 'inner', split_axis=0, concat_axis=2, tiled=True)]
  transfers between devices with their start and end apart: 3 -> 11, of which waited for: 1 -> 5; matrix products, arithmetic and copies ran while one was open for 1% -> 1% of each run, Pallas kernels for 0% -> 0%
where the time goes in v1:
time: 158 us; the launch traced here: 157 us
  blocking collectives  66.8 us (42%)
  waiting for transfers between devices  40.7 us (26%)
  starting transfers between devices  18 us (11%)
  between operations  13.6 us (9%)
  local copies, waits for them, and re-layouts  11.5 us (7%)
  matrix products  4.89 us (3%)
  other arithmetic  1.64 us (1%)
    all_to_all x1, blocking collectives, per_device(): lax.all_to_all(finish_state(running), 'outer', split_axis=0, concat_axis=...  17.9 us
    ppermute x7, waiting for transfers between devices, proceed_inputs(): ppermute(passed, comm_axis, [(p, (p + d) % t1) for p in range(t1)])  17.8 us
    all_to_all x1, blocking collectives, per_device(): lax.all_to_all(flatten(full_v), 'outer', split_axis=1, concat_axis=0, til...  17.2 us
    all_to_all x1, blocking collectives, per_device(): lax.all_to_all(values, 'inner', split_axis=0, concat_axis=2, tiled=True)  16.9 us
    all_to_all x1, blocking collectives, per_device(): lax.all_to_all(queries, 'inner', split_axis=0, concat_axis=2, tiled=True)  14.9 us
    all_to_all x1, waiting for transfers between devices, per_device(): lax.all_to_all(flatten(full_q), 'outer', split_axis=1, concat_axis=0, til...  14 us
    ppermute x7, starting transfers between devices, proceed_inputs(): ppermute(passed, comm_axis, [(p, (p + d) % t1) for p in range(t1)])  10.2 us
    all_to_all x1, waiting for transfers between devices, per_device(): lax.all_to_all(keys, 'inner', split_axis=0, concat_axis=2, tiled=True)  8.77 us
  transfers between devices with their start and end apart: 11, of which 5 were waited for; matrix products, arithmetic and copies ran while one was open for 1% of the time, Pallas kernels for 0%

profile of v1, /device:TPU:0, one launch (start us, length us, event | category | flops | bytes accessed | tf_op | source)
XLA Modules:
  0.0 157.4 jit_solution(2468502306638037459)
XLA Ops:
  6.5 4.3 %all-to-all-start = ((bf16[128,2,1024]{2,1,0:T(2,128)(2,1)}), bf16[128,2,1024]{2,1,0:T(2,128)(2,1)S(1)}, u32[]{:S(2)}, u32[]{:S(2)}) async-start(bf16[128,2,1024]{2,1,0:T(2,128)(2,1)} %param.6), calls=%async_computation | async-start | bytes 1048576 | tf_op jit(solution)/shard_map/all_to_all | solution.py:82
  10.8 8.8 %all-to-all-done = bf16[128,2,1024]{2,1,0:T(2,128)(2,1)S(1)} async-done(((bf16[128,2,1024]{2,1,0:T(2,128)(2,1)}), bf16[128,2,1024]{2,1,0:T(2,128)(2,1)S(1)}, u32[]{:S(2)}, u32[]{:S(2)}) %all-to-all-start) | async-done | bytes 524320 | tf_op jit(solution)/shard_map/all_to_all | solution.py:82
  19.8 5.2 %collective-permute-start.6 = (bf16[32,1024]{1,0:T(8,128)(2,1)S(1)}, bf16[32,1024]{1,0:T(8,128)(2,1)S(1)}, u32[]{:S(2)}, u32[]{:S(2)}) collective-permute-start(bf16[32,1024]{1,0:T(8,128)(2,1)S(1)} %get-tuple-element.103), channel_id=1, source_target_pairs={{0,28},{4,0},{8,4},{12,8},{16,12},{20,16},{24,20},{28,24},{1,29},{... | collective-permute-start | bytes 196616 | tf_op jit(solution)/shard_map/ppermute | solution.py:94
  25.5 3.0 %collective-permute-start.3 = (bf16[32,1024]{1,0:T(8,128)(2,1)S(1)}, bf16[32,1024]{1,0:T(8,128)(2,1)S(1)}, u32[]{:S(2)}, u32[]{:S(2)}) collective-permute-start(bf16[32,1024]{1,0:T(8,128)(2,1)S(1)} %get-tuple-element.106), channel_id=1, source_target_pairs={{0,16},{4,20},{8,24},{12,28},{16,0},{20,4},{24,8},{28,12},{1,17},{... | collective-permute-start | bytes 196616 | tf_op jit(solution)/shard_map/ppermute | solution.py:94
  28.5 1.5 collective-permute-start
  30.0 5.6 %collective-permute-done = bf16[32,1024]{1,0:T(8,128)(2,1)S(1)} collective-permute-done((bf16[32,1024]{1,0:T(8,128)(2,1)S(1)}, bf16[32,1024]{1,0:T(8,128)(2,1)S(1)}, u32[]{:S(2)}, u32[]{:S(2)}) %collective-permute-start) | collective-permute-done | bytes 65568 | tf_op jit(solution)/shard_map/ppermute | solution.py:94
  35.6 6.2 %collective-permute-done.1 = bf16[32,1024]{1,0:T(8,128)(2,1)S(1)} collective-permute-done((bf16[32,1024]{1,0:T(8,128)(2,1)S(1)}, bf16[32,1024]{1,0:T(8,128)(2,1)S(1)}, u32[]{:S(2)}, u32[]{:S(2)}) %collective-permute-start.1) | collective-permute-done | bytes 65568 | tf_op jit(solution)/shard_map/ppermute | solution.py:94
  41.8 6.1 %collective-permute-done.2 = bf16[32,1024]{1,0:T(8,128)(2,1)S(1)} collective-permute-done((bf16[32,1024]{1,0:T(8,128)(2,1)S(1)}, bf16[32,1024]{1,0:T(8,128)(2,1)S(1)}, u32[]{:S(2)}, u32[]{:S(2)}) %collective-permute-start.2) | collective-permute-done | bytes 65568 | tf_op jit(solution)/shard_map/ppermute | solution.py:94
  47.9 1.4 gather_fusion
  49.4 16.9 %all_to_all.93 = bf16[128,2,1024]{2,1,0:T(2,128)(2,1)S(1)} all-to-all(bf16[128,2,1024]{2,1,0:T(2,128)(2,1)S(1)} %copy-done), channel_id=1, replica_groups=mesh['outer'=8,'inner'=4] {'inner'}, dimensions={0} | all-to-all | bytes 1048576 | tf_op jit(solution)/shard_map/all_to_all | solution.py:83
  66.4 17.2 %all_to_all.94 = bf16[32,8,1024]{2,0,1:T(8,128)(2,1)} all-to-all(bf16[32,8,1024]{2,0,1:T(8,128)(2,1)S(1)} %bitcast.104), channel_id=1, replica_groups=mesh['outer'=8,'inner'=4] {'outer'}, dimensions={1} | all-to-all | bytes 1048576 | tf_op jit(solution)/shard_map/all_to_all | solution.py:102
  83.6 14.9 %all_to_all.95 = bf16[128,2,1024]{2,1,0:T(2,128)(2,1)S(1)} all-to-all(bf16[128,2,1024]{2,1,0:T(2,128)(2,1)S(1)} %copy-done.1), channel_id=1, replica_groups=mesh['outer'=8,'inner'=4] {'inner'}, dimensions={0} | all-to-all | bytes 1048576 | tf_op jit(solution)/shard_map/all_to_all | solution.py:81
  98.5 0.9 copy.17
  99.5 3.5 %all-to-all-start.2 = ((bf16[32,8,1024]{2,0,1:T(8,128)(2,1)}), bf16[32,8,1024]{2,0,1:T(8,128)(2,1)S(1)}, u32[]{:S(2)}, u32[]{:S(2)}) async-start(bf16[32,8,1024]{2,0,1:T(8,128)(2,1)} %bitcast.25), calls=%async_computation.2 | async-start | bytes 1048576 | tf_op jit(solution)/shard_map/all_to_all | solution.py:100
  103.0 14.0 %all-to-all-done.2 = bf16[32,8,1024]{2,0,1:T(8,128)(2,1)S(1)} async-done(((bf16[32,8,1024]{2,0,1:T(8,128)(2,1)}), bf16[32,8,1024]{2,0,1:T(8,128)(2,1)S(1)}, u32[]{:S(2)}, u32[]{:S(2)}) %all-to-all-start.2) | async-done | bytes 524320 | tf_op jit(solution)/shard_map/all_to_all | solution.py:100
  117.2 13.4 %while.15 = (s32[]{:T(128)}, f32[256,8]{0,1:T(8,128)S(1)}, f32[256,8]{0,1:T(8,128)S(1)}, f32[256,8,128]{0,2,1:T(8,128)S(1)}, bf16[4,256,1024]{2,1,0:T(8,128)(2,1...) while((s32[]{:T(128)}, f32[256,8]{0,1:T(8,128)S(1)}, ...), condition=%wide.region_3.4_spmd.clone, body=%wide.region_0.3_spmd.clone.sunk | while | flops 273426432 | bytes 14286965 | solution.py:57
  117.3 1.3 constant_dynamic-slice_fusion.3
  119.8 0.7 fusion.27
  120.6 1.3 constant_dynamic-slice_fusion.3
  123.2 0.7 fusion.27
  124.0 1.3 constant_dynamic-slice_fusion.3
  127.3 1.3 constant_dynamic-slice_fusion.3
  131.3 17.9 %all_to_all.96 = bf16[8,32,1024]{2,1,0:T(8,128)(2,1)S(1)} all-to-all(bf16[8,32,1024]{2,1,0:T(8,128)(2,1)S(1)} %convert_element_type.11), channel_id=1, replica_groups=mesh['outer'=8,'inner'=4] {'outer'}, dimensions={0} | all-to-all | bytes 1048576 | tf_op jit(solution)/shard_map/all_to_all | solution.py:114
  149.5 1.1 reshape.115
  (70 shorter events, 8.6 us)
Async XLA Ops:
  6.5 13.1 %all-to-all-start = ((bf16[128,2,1024]{2,1,0:T(2,128)(2,1)}), bf16[128,2,1024]{2,1,0:T(2,128)(2,1)S(1)}, u32[]{:S(2)}, u32[]{:S(2)}) async-start(bf16[128,2,1024]{2,1,0:T(2,128)(2,1)} %param.6), calls=%async_computation | async-start | bytes 1048576 | tf_op jit(solution)/shard_map/all_to_all | solution.py:82
  10.8 106.4 %all-gather.3.cloned.1.call-start = ((), (), s32[]{:S(2)}) async-start(), calls=%async_computation.6 | async-start | bytes 2621440 | tf_op jit(solution)/shard_map/all_gather | solution.py:109
  10.8 38.6 %copy-start = (bf16[128,2,1024]{2,1,0:T(2,128)(2,1)S(1)}, bf16[128,2,1024]{2,1,0:T(2,128)(2,1)}, u32[]{:S(2)}) copy-start(bf16[128,2,1024]{2,1,0:T(2,128)(2,1)} %param.7) | copy-start | bytes 1572868
  19.8 28.1 %collective-permute-start.6 = (bf16[32,1024]{1,0:T(8,128)(2,1)S(1)}, bf16[32,1024]{1,0:T(8,128)(2,1)S(1)}, u32[]{:S(2)}, u32[]{:S(2)}) collective-permute-start(bf16[32,1024]{1,0:T(8,128)(2,1)S(1)} %get-tuple-element.103), channel_id=1, source_target_pairs={{0,28},{4,0},{8,4},{12,8},{16,12},{20,16},{24,20},{28,24},{1,29},{... | collective-permute-start | bytes 196616 | tf_op jit(solution)/shard_map/ppermute | solution.py:94
  25.0 22.9 %collective-permute-start.5 = (bf16[32,1024]{1,0:T(8,128)(2,1)S(1)}, bf16[32,1024]{1,0:T(8,128)(2,1)S(1)}, u32[]{:S(2)}, u32[]{:S(2)}) collective-permute-start(bf16[32,1024]{1,0:T(8,128)(2,1)S(1)} %get-tuple-element.104), channel_id=1, source_target_pairs={{0,24},{4,28},{8,0},{12,4},{16,8},{20,12},{24,16},{28,20},{1,25},{... | collective-permute-start | bytes 196616 | tf_op jit(solution)/shard_map/ppermute | solution.py:94
  25.5 22.4 %collective-permute-start.4 = (bf16[32,1024]{1,0:T(8,128)(2,1)S(1)}, bf16[32,1024]{1,0:T(8,128)(2,1)S(1)}, u32[]{:S(2)}, u32[]{:S(2)}) collective-permute-start(bf16[32,1024]{1,0:T(8,128)(2,1)S(1)} %get-tuple-element.105), channel_id=1, source_target_pairs={{0,20},{4,24},{8,28},{12,0},{16,4},{20,8},{24,12},{28,16},{1,21},{... | collective-permute-start | bytes 196616 | tf_op jit(solution)/shard_map/ppermute | solution.py:94
  25.5 22.4 %collective-permute-start.3 = (bf16[32,1024]{1,0:T(8,128)(2,1)S(1)}, bf16[32,1024]{1,0:T(8,128)(2,1)S(1)}, u32[]{:S(2)}, u32[]{:S(2)}) collective-permute-start(bf16[32,1024]{1,0:T(8,128)(2,1)S(1)} %get-tuple-element.106), channel_id=1, source_target_pairs={{0,16},{4,20},{8,24},{12,28},{16,0},{20,4},{24,8},{28,12},{1,17},{... | collective-permute-start | bytes 196616 | tf_op jit(solution)/shard_map/ppermute | solution.py:94
  28.5 7.1 %collective-permute-start = (bf16[32,1024]{1,0:T(8,128)(2,1)S(1)}, bf16[32,1024]{1,0:T(8,128)(2,1)S(1)}, u32[]{:S(2)}, u32[]{:S(2)}) collective-permute-start(bf16[32,1024]{1,0:T(8,128)(2,1)S(1)} %get-tuple-element.109), channel_id=1, source_target_pairs={{0,4},{4,8},{8,12},{12,16},{16,20},{20,24},{24,28},{28,0},{1,5},{5... | collective-permute-start | bytes 196616 | tf_op jit(solution)/shard_map/ppermute | solution.py:94
  35.6 6.2 %collective-permute-start.1 = (bf16[32,1024]{1,0:T(8,128)(2,1)S(1)}, bf16[32,1024]{1,0:T(8,128)(2,1)S(1)}, u32[]{:S(2)}, u32[]{:S(2)}) collective-permute-start(bf16[32,1024]{1,0:T(8,128)(2,1)S(1)} %get-tuple-element.108), channel_id=1, source_target_pairs={{0,8},{4,12},{8,16},{12,20},{16,24},{20,28},{24,0},{28,4},{1,9},{5... | collective-permute-start | bytes 196616 | tf_op jit(solution)/shard_map/ppermute | solution.py:94
  41.8 6.1 %collective-permute-start.2 = (bf16[32,1024]{1,0:T(8,128)(2,1)S(1)}, bf16[32,1024]{1,0:T(8,128)(2,1)S(1)}, u32[]{:S(2)}, u32[]{:S(2)}) collective-permute-start(bf16[32,1024]{1,0:T(8,128)(2,1)S(1)} %get-tuple-element.107), channel_id=1, source_target_pairs={{0,12},{4,16},{8,20},{12,24},{16,28},{20,0},{24,4},{28,8},{1,13},{... | collective-permute-start | bytes 196616 | tf_op jit(solution)/shard_map/ppermute | solution.py:94
  49.3 34.3 %copy-start.1 = (bf16[128,2,1024]{2,1,0:T(2,128)(2,1)S(1)}, bf16[128,2,1024]{2,1,0:T(2,128)(2,1)}, u32[]{:S(2)}) copy-start(bf16[128,2,1024]{2,1,0:T(2,128)(2,1)} %param.5) | copy-start | bytes 1572868
  49.3 67.9 %all-gather.5.cloned.1.call-start = ((), (), s32[]{:S(2)}) async-start(), calls=%async_computation.7 | async-start | bytes 2621440 | tf_op jit(solution)/shard_map/all_gather | solution.py:110
  99.5 17.6 %all-to-all-start.2 = ((bf16[32,8,1024]{2,0,1:T(8,128)(2,1)}), bf16[32,8,1024]{2,0,1:T(8,128)(2,1)S(1)}, u32[]{:S(2)}, u32[]{:S(2)}) async-start(bf16[32,8,1024]{2,0,1:T(8,128)(2,1)} %bitcast.25), calls=%async_computation.2 | async-start | bytes 1048576 | tf_op jit(solution)/shard_map/all_to_all | solution.py:100
Sparse Core Ops, SparseCore 0:
  49.5 24.0 all-gather.2
  83.8 23.8 all-gather.4
